TPU v7x, 32 devices: a whole 2x2x4 slice. The times are simulated.
32 devices in a mesh: feat: 8 (over y, x, core), rep: 4 (over z).
Axes of the slice: x: 2, y: 2, z: 4, core: 2. Of those that a mesh axis runs over, the one named last changes fastest.
Arguments:
- features: bfloat16 [4, 8, 1024, 512], P('rep', None, 'feat'), may hold values from -6 to 6
- adjacency_one: int32 [4, 8, 5, 16, 512], P('rep'), may hold values from 0 to 65535, as said below
- pre_hidden: bfloat16 [4, 8, 256, 256], P('rep', 'feat'), may hold values from -6 to 6
- adjacency_two: int32 [4, 8, 5, 8, 256], P('rep', 'feat'), may hold values from 0 to 65535, as said below
- weight_two: bfloat16 [6, 256, 256], replicated, may hold values from -0.375 to 0.375
- out_grad: bfloat16 [4, 8, 128, 256], P('rep', 'feat'), may hold values from -6 to 6
Outputs:
- grad_w1: float32 [6, 1024, 256], P(None, 'feat')
- grad_b1: float32 [256], replicated
- grad_w2: float32 [6, 256, 256], replicated
- grad_b2: float32 [256], replicated
Inputs may be any that keep to these rules, and one draw needn't show every extreme that they name: `adjacency_one`: bit k, k below 16, of word (w, n) is the entry of destination row 16 w + k and source column n; higher bits are zero; some rows are empty. `adjacency_two`: bit k, k below 16, of word (w, n) is the entry of seed row 16 w + k and source column n; higher bits are zero; some rows are empty.
All inputs are finite; a program needn't handle non-finite values.
Results may differ from a plain program's by a relative error of at most 0.0041.
Values may be sent and summed in bfloat16 or wider, within the bound.
No kernel may reach another device: no remote copies, remote signals or barrier semaphores. Data moves between devices by JAX's collectives and lax.ppermute only.
A program may use at most 128 MiB of HBM per device.

v0:
```python
import math
import jax
import jax.numpy as jnp
from jax import lax
from jax.sharding import PartitionSpec as P


def unpack(packed):
    shifts = jnp.arange(16, dtype=jnp.int32)
    spread = jnp.bitwise_and(jnp.right_shift(packed[..., None, :], shifts[:, None]), 1)
    dense = spread.reshape(packed.shape[:-2] + (packed.shape[-2] * 16, packed.shape[-1]))
    degree = jnp.sum(dense, axis=-1).astype(jnp.float32)
    return (dense.astype(jnp.bfloat16), 1.0 / jnp.maximum(degree, 1.0))


def upper_layer(pre_rows, words_two, grad_rows, weight_two, factor):
    hidden = jnp.maximum(pre_rows, 0)
    seed_count = grad_rows.shape[0]
    matrix, inverse = unpack(words_two)
    mixed = (
        jnp.einsum("rsd,dh->rsh", matrix, hidden, preferred_element_type=jnp.float32)
        * inverse[..., None]
    ).astype(jnp.bfloat16)
    scaled = grad_rows.astype(jnp.float32) * factor
    scaled_low = scaled.astype(jnp.bfloat16)
    grad_rel = jnp.einsum("rsh,sk->rhk", mixed, scaled_low, preferred_element_type=jnp.float32)
    grad_self = jnp.einsum(
        "sh,sk->hk", hidden[:seed_count], scaled_low, preferred_element_type=jnp.float32
    )
    weight_grad = jnp.concatenate([grad_self[None], grad_rel], 0)
    backed = (
        jnp.einsum("sk,rhk->rsh", scaled_low, weight_two[1:], preferred_element_type=jnp.float32)
        * inverse[..., None]
    ).astype(jnp.bfloat16)
    spread_back = jnp.einsum("rsd,rsh->dh", matrix, backed, preferred_element_type=jnp.float32)
    own_part = jnp.einsum(
        "sk,hk->sh", scaled_low, weight_two[0], preferred_element_type=jnp.float32
    )
    hidden_total = spread_back + jnp.pad(own_part, ((0, hidden.shape[0] - seed_count), (0, 0)))
    hidden_grad = jnp.where(pre_rows > 0, hidden_total, 0.0).astype(jnp.bfloat16)
    return (
        weight_grad,
        jnp.sum(scaled, 0),
        hidden_grad,
        jnp.sum(hidden_grad.astype(jnp.float32), 0),
    )


def panel_terms(word_block, column_block, grad_block):
    matrix, inverse = unpack(word_block)
    rows_one = grad_block.shape[1]
    gathered = (
        jnp.einsum("brdn,bcn->brdc", matrix, column_block, preferred_element_type=jnp.float32)
        * inverse[..., None]
    ).astype(jnp.bfloat16)
    panel_rel = jnp.einsum(
        "brdc,bdh->rch", gathered, grad_block, preferred_element_type=jnp.float32
    )
    panel_self = jnp.einsum(
        "bcd,bdh->ch", column_block[:, :, :rows_one], grad_block, preferred_element_type=jnp.float32
    )
    return jnp.concatenate([panel_self[None], panel_rel], 0)


def on_device(features, adjacency_one, pre_hidden, adjacency_two, weight_two, out_grad):
    seed_count = out_grad.shape[2]
    factor = float(seed_count * lax.axis_size("feat") * lax.axis_size("rep")) ** (-0.5)
    weight_grad, bias_two, hidden_grad, bias_one = upper_layer(
        pre_hidden[0, 0], adjacency_two[0, 0], out_grad[0, 0], weight_two, factor
    )
    feature_local = features[0]
    adj_local = adjacency_one[0]
    col_width = feature_local.shape[1]
    hidden_width = hidden_grad.shape[1]
    relations = adj_local.shape[1]
    initial = jnp.zeros((relations + 1, col_width, hidden_width), jnp.float32)
    piece = lax.all_gather(hidden_grad[None], "feat", axis=0, tiled=True)
    piece_rows = piece.shape[0]
    group_size = math.gcd(piece_rows, 8)
    turn_count = piece_rows // group_size
    word_block = adj_local
    word_block = word_block.reshape((turn_count, group_size) + adj_local.shape[1:])
    column_block = feature_local
    column_block = column_block.reshape((turn_count, group_size) + feature_local.shape[1:])
    grad_block = piece.reshape((turn_count, group_size) + piece.shape[1:])

    def one_turn(running, inputs):
        return (running + panel_terms(inputs[0], inputs[1], inputs[2]), None)

    running, unused = lax.scan(one_turn, initial, (word_block, column_block, grad_block))
    grad_w1 = lax.psum(running, "rep")
    grad_w2, grad_b1, grad_b2 = lax.psum((weight_grad, bias_one, bias_two), ("feat", "rep"))
    return (grad_w1, grad_b1, grad_w2, grad_b2)


def solution(mesh):
    placed = (
        P("rep", None, "feat", None),
        P("rep", None, None, None, None),
        P("rep", "feat", None, None),
        P("rep", "feat", None, None, None),
        P(),
        P("rep", "feat", None, None),
    )
    return jax.shard_map(
        on_device,
        mesh=mesh,
        in_specs=placed,
        out_specs=(P(None, "feat", None), P(), P(), P()),
        check_vma=False,
    )
```

profile of v0, /device:TPU:0, one launch (start us, length us, event | category | flops | bytes accessed | tf_op | source)
XLA Modules:
  0.0 213.1 jit_solution(5158156742498113044)
XLA Ops:
  8.0 0.0 copy-start
  8.0 0.0 all-gather.3.cloned.1.call-start
  8.1 1.6 fusion.28
  9.7 0.1 div.22
  9.8 0.1 shift_right_arithmetic.72
  9.9 0.9 fusion.27
  10.8 1.1 fusion.37
  11.9 2.4 %convert_reduce_fusion = (f32[256]{0:T(256)S(1)}, bf16[256,256]{1,0:T(8,128)(2,1)}) fusion(f32[128,256]{1,0:T(8,128)S(1)} %fusion.37, bf16[5,128,256]{2,1,0:T(8,128)(2,1)S(1)} %fusion.27, bf16[6,256,256]{2,1,0:T(8,128)(2,1)} %param.10, f32[5,128]{1,0:T(8,128)S(1)} %div.22, bf16[1,1,128,256]{3,2,1,0:T(8,128)(2,1)} %param.11, bf16[1,1,256,256]{3,2,1,0:T(8,128)(2,1)} %param.8), kind=kOutput, calls=%fused_computation.38 | convolution fusion | flops 168722176 | bytes 1445376 | tf_op jit(solution)/shard_map/rsd,rsh->dh/dot_general | solution.py:35
  14.4 0.0 all-gather.3.cloned.1.call-update
  14.4 0.0 all-reduce.7.cloned.1.call-start
  14.4 0.9 broadcast_maximum_fusion
  15.4 1.0 convolution_bitcast_fusion.1
  16.4 1.6 fusion.19
  18.0 1.2 pad_maximum_fusion
  19.3 0.0 all-reduce.7.cloned.1.call-update
  19.3 0.2 all-reduce.5.cloned.1.call-start
  19.5 0.0 copy-done
  19.5 10.9 %and_reduce_fusion = s32[8,5,16,16]{3,2,1,0:T(8,128)S(1)} fusion(s32[8,5,16,512]{3,2,1,0:T(8,128)S(1)} %bitcast.90), kind=kLoop, calls=%fused_computation.3 | loop fusion | flops 15718400 | bytes 1351680 | tf_op jit(solution)/shard_map/while/body/eval_jaxpr/reduce_sum | solution.py:12
  30.4 0.1 maximum_divide_fusion
  30.5 0.2 reshape.90
  30.7 0.1 shift_right_arithmetic.81
  30.7 10.1 %all-gather.3.cloned.1.call-done = bf16[2048,256]{1,0:T(8,128)(2,1)} async-done(((bf16[256,256]{1,0:T(8,128)(2,1)}), bf16[2048,256]{1,0:T(8,128)(2,1)}) %all-gather.3.cloned.1.call-update) | async-done | bytes 1048592 | tf_op jit(solution)/shard_map/all_gather | solution.py:77
  40.9 0.0 copy-start.2
  40.9 0.0 copy-start.3
  40.9 10.5 %shift_right_arithmetic.78 = s32[8,5,16,16,512]{4,3,2,1,0:T(8,128)} broadcast(s32[8,5,16,512]{3,2,1,0:T(8,128)S(1)} %bitcast.91), dimensions={0,1,2,4} | broadcast | bytes 22282240 | tf_op jit(solution)/shard_map/while/body/eval_jaxpr/shift_right_arithmetic | solution.py:10
  51.3 0.0 copy-done.2
  51.3 0.0 copy-done.3
  51.3 0.0 copy-start.1
  51.3 9.5 %fusion.13 = f32[5,128,256]{2,1,0:T(8,128)S(1)} fusion(bf16[8,256,256,1]{2,1,0,3:T(8,128)(2,1)S(1)} %bitcast.96, f32[8,5,256]{2,0,1:T(8,128)S(1)} %copy.37, s32[8,5,256,512]{3,2,1,0:T(8,128)} %bitcast.89, s32[256]{0:T(256)S(1)} %shift_right_arithmetic.81, bf16[1,8,128,512]{3,2,1,0:T(8,128)(2,1)S(1)} %copy-done.2), kind=kOutput, calls=%fused_computation.14 | convolution fusion | flops 2031616000 | bytes 23766016 | tf_op jit(solution)/shard_map/while/body/eval_jaxpr/brdc,bdh->rch/dot_general | solution.py:56
  60.8 0.5 convolution_bitcast_fusion.2
  61.3 0.1 copy.30
  61.4 1.0 pad_maximum_fusion.1
  62.4 0.0 all-reduce.5.cloned.1.call-update
  62.4 0.0 copy-done.1
  62.4 39.3 %all-reduce.1 = (f32[256]{0:T(256)}, f32[256]{0:T(256)}) all-reduce(f32[256]{0:T(256)S(1)} %get-tuple-element.23, f32[256]{0:T(256)S(1)} %fusion.40), channel_id=1, replica_groups=mesh['feat'=8,'rep'=4] {'feat','rep'}, use_global_device_ids=true, to_apply=%region_4.5 | all-reduce | flops 512 | bytes 4096 | tf_op jit(solution)/shard_map/psum | solution.py:92
  101.8 53.7 %all-reduce.7.cloned.1.call-done = f32[6,256,256]{2,1,0:T(8,128)} async-done(((f32[6,256,256]{2,1,0:T(8,128)}), f32[6,256,256]{2,1,0:T(8,128)}) %all-reduce.7.cloned.1.call-update) | async-done | bytes 1572880 | tf_op jit(solution)/shard_map/psum | solution.py:92
  155.4 45.4 %all-reduce.5.cloned.1.call-done = f32[6,128,256]{2,1,0:T(8,128)} async-done(((f32[6,128,256]{2,1,0:T(8,128)}), f32[6,128,256]{2,1,0:T(8,128)}) %all-reduce.5.cloned.1.call-update) | async-done | bytes 786448 | tf_op jit(solution)/shard_map/psum | solution.py:91
  200.8 2.1 copy.52
  202.9 2.7 %copy.53 = f32[6,256,256]{2,1,0:T(8,128)} copy(f32[6,256,256]{2,1,0:T(8,128)} %all-reduce.7.cloned.1.call-done) | data formatting | bytes 3145728
  (5 shorter events, 0.1 us)
Async XLA Ops:
  8.0 11.5 %copy-start = (s32[1,8,5,16,512]{4,3,2,1,0:T(8,128)S(1)}, s32[1,8,5,16,512]{4,3,2,1,0:T(8,128)}, u32[]{:S(2)}) copy-start(s32[1,8,5,16,512]{4,3,2,1,0:T(8,128)} %param.7) | copy-start | bytes 3932164
  8.0 32.9 %all-gather.3.cloned.1.call-start = ((), (), s32[]{:S(2)}) async-start(), calls=%async_computation.2 | async-start | bytes 1179648 | tf_op jit(solution)/shard_map/all_gather | solution.py:77
  14.4 141.0 %all-reduce.7.cloned.1.call-start = ((), (), s32[]{:S(2)}) async-start(), calls=%async_computation.1 | async-start | bytes 3145728 | tf_op jit(solution)/shard_map/psum | solution.py:92
  19.3 181.5 %all-reduce.5.cloned.1.call-start = ((), (), s32[]{:S(2)}) async-start(), calls=%async_computation | async-start | bytes 1572864 | tf_op jit(solution)/shard_map/psum | solution.py:91
  40.9 10.5 %copy-start.2 = (bf16[1,8,128,512]{3,2,1,0:T(8,128)(2,1)S(1)}, bf16[1,8,128,512]{3,2,1,0:T(8,128)(2,1)}, u32[]{:S(2)}) copy-start(bf16[1,8,128,512]{3,2,1,0:T(8,128)(2,1)} %param.6) | copy-start | bytes 3145732
  40.9 10.5 %copy-start.3 = (bf16[2048,256]{1,0:T(8,128)(2,1)S(1)}, bf16[2048,256]{1,0:T(8,128)(2,1)}, u32[]{:S(2)}) copy-start(bf16[2048,256]{1,0:T(8,128)(2,1)} %all-gather.3.cloned.1.call-done) | copy-start | bytes 3145732
  51.3 11.0 %copy-start.1 = (bf16[1,1,128,256]{3,2,1,0:T(8,128)(2,1)S(1)}, bf16[1,1,128,256]{3,2,1,0:T(8,128)(2,1)}, u32[]{:S(2)}) copy-start(bf16[1,1,128,256]{3,2,1,0:T(8,128)(2,1)} %param.11) | copy-start | bytes 196612
Sparse Core Ops, SparseCore 0:
  14.5 26.3 all-gather.2
Sparse Core Ops, SparseCore 1:
  20.7 134.6 all-reduce.6
  158.2 42.5 all-reduce.4
where the time goes:
time: 214 us; the launch traced here: 213 us
  waiting for transfers between devices  109 us (51%)
  blocking collectives  39.3 us (18%)
  other arithmetic  16.6 us (8%)
  matrix products  16.1 us (8%)
  local copies, waits for them, and re-layouts  15.8 us (7%)
  between operations  15.6 us (7%)
    psum x1, waiting for transfers between devices, on_device(): lax.psum((weight_grad, bias_one, bias_two), ('feat', 'rep'))  53.7 us
    psum x1, waiting for transfers between devices, on_device(): grad_w1 = lax.psum(running, 'rep')  45.4 us
    psum x1, blocking collectives, on_device(): lax.psum((weight_grad, bias_one, bias_two), ('feat', 'rep'))  39.3 us
    reduce_sum x1, other arithmetic, unpack(): degree = jnp.sum(dense, axis=-1).astype(jnp.float32)  10.9 us
    shift_right_arithmetic x5, local copies, waits for them, and re-layouts, unpack(): jnp.right_shift(packed[..., None, :], shifts[:, None])  10.6 us
    all_gather x1, waiting for transfers between devices, on_device(): piece = lax.all_gather(hidden_grad[None], 'feat', axis=0, tiled=True)  10.1 us
    dot_general x1, matrix products, panel_terms(): jnp.einsum('brdc,bdh->rch', gathered, grad_block, preferred_element_type=...  9.46 us
    unnamed x10, local copies, waits for them, and re-layouts  4.85 us
  transfers between devices with their start and end apart: 3, of which 3 were waited for; matrix products, arithmetic and copies ran while one was open for 18% of the time, Pallas kernels for 0%

commit v1 on v0

--- a/solution.py
+++ b/solution.py
@@ -63,6 +63,12 @@
 
 
 def on_device(features, adjacency_one, pre_hidden, adjacency_two, weight_two, out_grad):
+
+    def save_values_on_mesh(raw):
+        for jj in ("rep", "feat"):
+            raw = lax.psum(raw, axis_name=jj)
+        return raw
+
     seed_count = out_grad.shape[2]
     factor = float(seed_count * lax.axis_size("feat") * lax.axis_size("rep")) ** (-0.5)
     weight_grad, bias_two, hidden_grad, bias_one = upper_layer(
@@ -89,7 +95,7 @@
 
     running, unused = lax.scan(one_turn, initial, (word_block, column_block, grad_block))
     grad_w1 = lax.psum(running, "rep")
-    grad_w2, grad_b1, grad_b2 = lax.psum((weight_grad, bias_one, bias_two), ("feat", "rep"))
+    grad_w2, grad_b1, grad_b2 = save_values_on_mesh((weight_grad, bias_one, bias_two))
     return (grad_w1, grad_b1, grad_w2, grad_b2)
 
 

time: 214 us -> 229 us (1.070)
  waiting for transfers between devices: 109 us -> 145 us
  blocking collectives: 39.3 us -> 22.5 us
    psum x1, waiting for transfers between devices: 45.4 us -> 94.7 us  [on_device(): grad_w1 = lax.psum(running, 'rep')]
    psum x1 -> x2, blocking collectives: 39.3 us -> 22.5 us  [save_values_on_mesh(): raw = lax.psum(raw, axis_name=jj)]
    psum x1, waiting for transfers between devices: 53.7 us -> 38.6 us  [save_values_on_mesh(): raw = lax.psum(raw, axis_name=jj)]
  transfers between devices with their start and end apart: 3 -> 3, of which waited for: 3 -> 3; matrix products, arithmetic and copies ran while one was open for 18% -> 7% of each run, Pallas kernels for 0% -> 0%
where the time goes in v1:
time: 229 us
  waiting for transfers between devices  145 us (63%)
  blocking collectives  22.5 us (10%)
  other arithmetic  17.2 us (8%)
  matrix products  15.8 us (7%)
  local copies, waits for them, and re-layouts  15 us (7%)
  between operations  13.9 us (6%)
    psum x1, waiting for transfers between devices, on_device(): grad_w1 = lax.psum(running, 'rep')  94.7 us
    psum x1, waiting for transfers between devices, save_values_on_mesh(): raw = lax.psum(raw, axis_name=jj)  38.6 us
    psum x2, blocking collectives, save_values_on_mesh(): raw = lax.psum(raw, axis_name=jj)  22.5 us
    reduce_sum x1, other arithmetic, unpack(): degree = jnp.sum(dense, axis=-1).astype(jnp.float32)  12.3 us
    all_gather x1, waiting for transfers between devices, on_device(): piece = lax.all_gather(hidden_grad[None], 'feat', axis=0, tiled=True)  11.1 us
    shift_right_arithmetic x5, local copies, waits for them, and re-layouts, unpack(): jnp.right_shift(packed[..., None, :], shifts[:, None])  9.83 us
    dot_general x1, matrix products, panel_terms(): jnp.einsum('brdc,bdh->rch', gathered, grad_block, preferred_element_type=...  9.39 us
    unnamed x10, local copies, waits for them, and re-layouts  4.86 us
  transfers between devices with their start and end apart: 3, of which 3 were waited for; matrix products, arithmetic and copies ran while one was open for 7% of the time, Pallas kernels for 0%

profile of v1, /device:TPU:0, one launch (start us, length us, event | category | flops | bytes accessed | tf_op | source)
XLA Modules:
  0.0 229.1 jit_solution(9579017979459728806)
XLA Ops:
  7.2 0.0 copy-start.1
  7.2 0.0 copy-start.2
  7.2 0.0 all-gather.3.cloned.1.call-start
  7.2 1.6 fusion.28
  8.8 0.1 div.22
  8.9 0.1 shift_right_arithmetic.72
  9.0 0.9 fusion.27
  9.9 1.1 fusion.37
  11.1 2.4 %convert_reduce_fusion = (f32[256]{0:T(256)S(1)}, bf16[256,256]{1,0:T(8,128)(2,1)}) fusion(f32[128,256]{1,0:T(8,128)S(1)} %fusion.37, bf16[5,128,256]{2,1,0:T(8,128)(2,1)S(1)} %fusion.27, bf16[6,256,256]{2,1,0:T(8,128)(2,1)} %param.10, f32[5,128]{1,0:T(8,128)S(1)} %div.22, bf16[1,1,128,256]{3,2,1,0:T(8,128)(2,1)} %param.11, bf16[1,1,256,256]{3,2,1,0:T(8,128)(2,1)} %param.8), kind=kOutput, calls=%fused_computation.38 | convolution fusion | flops 168722176 | bytes 1445376 | tf_op jit(solution)/shard_map/rsd,rsh->dh/dot_general | solution.py:35
  13.5 0.0 all-gather.3.cloned.1.call-update
  13.5 0.0 copy-start
  13.5 0.0 all-reduce.9.cloned.1.call-start
  13.6 12.3 %and_reduce_fusion = s32[8,5,16,16]{3,2,1,0:T(8,128)S(1)} fusion(s32[8,5,16,512]{3,2,1,0:T(8,128)} %bitcast.90), kind=kLoop, calls=%fused_computation.3 | loop fusion | flops 15718400 | bytes 1351680 | tf_op jit(solution)/shard_map/while/body/eval_jaxpr/reduce_sum | solution.py:12
  25.9 0.1 maximum_divide_fusion
  25.9 0.2 reshape.90
  26.1 0.1 shift_right_arithmetic.81
  26.2 0.0 copy-done.2
  26.2 0.0 copy-done.1
  26.2 0.2 convolution_bitcast_fusion.1
  26.4 0.9 fusion.19
  27.3 1.3 pad_maximum_fusion
  28.6 11.1 %all-gather.3.cloned.1.call-done = bf16[2048,256]{1,0:T(8,128)(2,1)} async-done(((bf16[256,256]{1,0:T(8,128)(2,1)}), bf16[2048,256]{1,0:T(8,128)(2,1)}) %all-gather.3.cloned.1.call-update) | async-done | bytes 1048592 | tf_op jit(solution)/shard_map/all_gather | solution.py:83
  39.8 1.8 convolution_bitcast_fusion.2
  41.6 0.1 copy.30
  41.7 0.0 copy-done
  41.7 0.0 copy-start.3
  41.7 9.7 %shift_right_arithmetic.78 = s32[8,5,16,16,512]{4,3,2,1,0:T(8,128)} broadcast(s32[8,5,16,512]{3,2,1,0:T(8,128)S(1)} %bitcast.91), dimensions={0,1,2,4} | broadcast | bytes 22282240 | tf_op jit(solution)/shard_map/while/body/eval_jaxpr/shift_right_arithmetic | solution.py:10
  51.4 0.0 copy-done.3
  51.4 9.4 %fusion.13 = f32[5,128,256]{2,1,0:T(8,128)S(1)} fusion(bf16[8,256,256,1]{2,1,0,3:T(8,128)(2,1)} %bitcast.97, f32[8,5,256]{2,0,1:T(8,128)S(1)} %copy.37, s32[8,5,256,512]{3,2,1,0:T(8,128)} %bitcast.89, s32[256]{0:T(256)S(1)} %shift_right_arithmetic.81, bf16[1,8,128,512]{3,2,1,0:T(8,128)(2,1)S(1)} %copy-done.3), kind=kOutput, calls=%fused_computation.14 | convolution fusion | flops 2031616000 | bytes 23766016 | tf_op jit(solution)/shard_map/while/body/eval_jaxpr/brdc,bdh->rch/dot_general | solution.py:56
  60.8 0.9 pad_maximum_fusion.1
  61.7 0.0 all-reduce.9.cloned.1.call-update
  61.7 0.0 all-reduce.7.cloned.1.call-start
  61.8 94.7 %all-reduce.9.cloned.1.call-done = (f32[6,128,256]{2,1,0:T(8,128)}, f32[6,256,256]{2,1,0:T(8,128)}) async-done(((f32[6,128,256]{2,1,0:T(8,128)}, f32[6,256,256]{2,1,0:T(8,128)}), (f32[6,128,256]{2,1,0:T(8,128)}, f32[6,256,256]{2,1,0:T(8,128)})) %all-reduce.9.cloned.1.call-update) | async-done | bytes 2359312 | tf_op jit(solution)/shard_map/psum | solution.py:97
  156.5 0.0 all-reduce.7.cloned.1.call-update
  156.6 10.0 %all-reduce.2 = (f32[256]{0:T(256)S(1)}, f32[256]{0:T(256)S(1)}) all-reduce(f32[256]{0:T(256)S(1)} %get-tuple-element.27, f32[256]{0:T(256)S(1)} %fusion.40), channel_id=1, replica_groups=mesh['feat'=8,'rep'=4] {'rep'}, use_global_device_ids=true, to_apply=%region_4.5 | all-reduce | flops 512 | bytes 4096 | tf_op jit(solution)/shard_map/psum | solution.py:69
  166.6 12.5 %all-reduce.1 = (f32[256]{0:T(256)}, f32[256]{0:T(256)}) all-reduce(f32[256]{0:T(256)S(1)} %get-tuple-element.21, f32[256]{0:T(256)S(1)} %get-tuple-element.22), channel_id=1, replica_groups=mesh['feat'=8,'rep'=4] {'feat'}, use_global_device_ids=true, to_apply=%region_5.6 | all-reduce | flops 512 | bytes 4096 | tf_op jit(solution)/shard_map/psum | solution.py:69
  179.1 38.6 %all-reduce.7.cloned.1.call-done = f32[6,256,256]{2,1,0:T(8,128)} async-done(((f32[6,256,256]{2,1,0:T(8,128)}), f32[6,256,256]{2,1,0:T(8,128)}) %all-reduce.7.cloned.1.call-update) | async-done | bytes 1572880 | tf_op jit(solution)/shard_map/psum | solution.py:69
  217.7 2.1 copy.53
  219.8 2.7 %copy.54 = f32[6,256,256]{2,1,0:T(8,128)} copy(f32[6,256,256]{2,1,0:T(8,128)} %all-reduce.7.cloned.1.call-done) | data formatting | bytes 3145728
  (6 shorter events, 0.1 us)
Async XLA Ops:
  7.2 19.1 %copy-start.1 = (bf16[1,1,128,256]{3,2,1,0:T(8,128)(2,1)S(1)}, bf16[1,1,128,256]{3,2,1,0:T(8,128)(2,1)}, u32[]{:S(2)}) copy-start(bf16[1,1,128,256]{3,2,1,0:T(8,128)(2,1)} %param.11) | copy-start | bytes 196612
  7.2 19.0 %copy-start.2 = (bf16[1,1,256,256]{3,2,1,0:T(8,128)(2,1)S(1)}, bf16[1,1,256,256]{3,2,1,0:T(8,128)(2,1)}, u32[]{:S(2)}) copy-start(bf16[1,1,256,256]{3,2,1,0:T(8,128)(2,1)} %param.8) | copy-start | bytes 393220
  7.2 32.6 %all-gather.3.cloned.1.call-start = ((), (), s32[]{:S(2)}) async-start(), calls=%async_computation.1 | async-start | bytes 1179648 | tf_op jit(solution)/shard_map/all_gather | solution.py:83
  13.5 28.2 %copy-start = (s32[1,8,5,16,512]{4,3,2,1,0:T(8,128)S(1)}, s32[1,8,5,16,512]{4,3,2,1,0:T(8,128)}, u32[]{:S(2)}) copy-start(s32[1,8,5,16,512]{4,3,2,1,0:T(8,128)} %param.7) | copy-start | bytes 3932164
  13.5 143.0 %all-reduce.9.cloned.1.call-start = ((), (), s32[]{:S(2)}) async-start(), calls=%async_computation.2 | async-start | bytes 4718592 | tf_op jit(solution)/shard_map/psum | solution.py:97
  41.7 9.7 %copy-start.3 = (bf16[1,8,128,512]{3,2,1,0:T(8,128)(2,1)S(1)}, bf16[1,8,128,512]{3,2,1,0:T(8,128)(2,1)}, u32[]{:S(2)}) copy-start(bf16[1,8,128,512]{3,2,1,0:T(8,128)(2,1)} %param.6) | copy-start | bytes 3145732
  61.7 156.0 %all-reduce.7.cloned.1.call-start = ((), (), s32[]{:S(2)}) async-start(), calls=%async_computation | async-start | bytes 3145728 | tf_op jit(solution)/shard_map/psum | solution.py:69
Sparse Core Ops, SparseCore 0:
  13.6 26.0 all-gather.2
  61.9 94.6 all-reduce.8
  159.8 57.8 all-reduce.6
